TPU v7x, 32 devices: a whole 2x2x4 slice. The times are simulated.
32 devices in a mesh: dp: 8 (over y, x, core), tensor: 4 (over z).
Axes of the slice: x: 2, y: 2, z: 4, core: 2. Of those that a mesh axis runs over, the one named last changes fastest.
Arguments:
- tokens: bfloat16 [6400, 1024], P('dp'), may hold values from -10.5 to 10.5, as said below
- blank_mask: int32 [64], P('dp'), may hold values 0 or 1
- norm_gain: float32 [2, 1024], replicated, may hold values from 0.25 to 1.75
- norm_bias: float32 [2, 1024], replicated, may hold values from -1.8 to 1.8
- w_qkv: bfloat16 [3, 1024, 1024], P(None, None, 'tensor'), may hold values from -0.1875 to 0.1875
- qv_bias: float32 [2, 1024], P(None, 'tensor'), may hold values from -1.8 to 1.8
- rel_bias: float32 [32, 361], P('tensor'), may hold values from -5 to 5
- w_out: bfloat16 [1024, 1024], P('tensor'), may hold values from -0.75 to 0.75
- out_bias: float32 [2, 1024], replicated, may hold values from -1.8 to 1.8
- w_up: bfloat16 [1024, 4096], P(None, 'tensor'), may hold values from -0.1875 to 0.1875
- up_bias: float32 [4096], P('tensor'), may hold values from -1.8 to 1.8
- w_down: bfloat16 [4096, 1024], P('tensor'), may hold values from -0.09375 to 0.09375
- grad_out: bfloat16 [6400, 1024], P('dp'), may hold values from -6 to 6
Outputs:
- output: bfloat16 [6400, 1024], P(('dp', 'tensor'))
- grad_tokens: float32 [6400, 1024], P(('dp', 'tensor'))
- grad_norm_gain: float32 [2, 1024], replicated
- grad_norm_bias: float32 [2, 1024], replicated
- grad_w_qkv: float32 [3, 1024, 1024], P(None, None, 'tensor')
- grad_qv_bias: float32 [2, 1024], P(None, 'tensor')
- grad_rel_bias: float32 [32, 361], P('tensor')
- grad_w_out: float32 [1024, 1024], P('tensor')
- grad_out_bias: float32 [2, 1024], replicated
- grad_w_up: float32 [1024, 4096], P(None, 'tensor')
- grad_up_bias: float32 [4096], P('tensor')
- grad_w_down: float32 [4096, 1024], P('tensor')
- root_means: float32 [3], replicated
Inputs may be any that keep to these rules, and one draw needn't show every extreme that they name: `tokens`: values are of order one, with row scales differing between windows. `blank_mask`: 1 marks a blank window.
All inputs are finite; a program needn't handle non-finite values. No bound on the sum of `blank_mask` on one device may be relied on, other than what follows from the above.
Results may differ from a plain program's by a relative error of at most 0.0095.
The roundings to bfloat16 on the way count: a program that leaves them out, or rounds other values in their place, can miss the bound.
Values may be sent and summed in bfloat16 or wider, within the bound.
A program may use at most 128 MiB of HBM per device.

v0:
```python
import jax
import jax.numpy as jnp
from jax import lax
from jax.sharding import PartitionSpec as P

WS = 10
highest = lax.Precision.HIGHEST
norm_eps = 1e-05
half_root = 0.7071067811865476
gauss_norm = 0.3989422804014327


def normalize(values):
    center = jnp.mean(values, axis=-1, keepdims=True)
    shifted = values - center
    spread = jnp.mean(shifted * shifted, axis=-1, keepdims=True)
    inverse = lax.rsqrt(spread + norm_eps)
    return (shifted * inverse, inverse)


def norm_back(gradient, normed_hat, inverse, gain_row):
    scaled = gradient * gain_row
    inner_sum = jnp.mean(scaled, axis=-1, keepdims=True)
    cross_sum = jnp.mean(scaled * normed_hat, axis=-1, keepdims=True)
    return inverse * (scaled - inner_sum - normed_hat * cross_sum)


def relative_onehot(window_side):
    positions = jnp.arange(window_side)
    offset_grid = positions[:, None] - positions[None, :] + (window_side - 1)
    return (offset_grid[:, :, None] == jnp.arange(2 * window_side - 1)[None, None, :]).astype(
        jnp.float32
    )


def relative(bias_table, window_side):
    onehot = relative_onehot(window_side)
    heads_count = bias_table.shape[0]
    square = bias_table.reshape(heads_count, 2 * window_side - 1, 2 * window_side - 1)
    spread_full = jnp.einsum("ija,klb,hab->hikjl", onehot, onehot, square, precision=highest)
    return spread_full.reshape(heads_count, window_side * window_side, window_side * window_side)


def relative_back(gradient, window_side):
    onehot = relative_onehot(window_side)
    heads_count = gradient.shape[0]
    grad_grid = gradient.reshape(heads_count, window_side, window_side, window_side, window_side)
    folded = jnp.einsum("hikjl,ija,klb->hab", grad_grid, onehot, onehot, precision=highest)
    return folded.reshape(heads_count, (2 * window_side - 1) ** 2)


def scatter_rows(part):
    sums = lax.psum_scatter(part.astype(jnp.bfloat16), "tensor", scatter_dimension=0, tiled=True)
    return sums.astype(jnp.float32)


def on_device(
    tokens,
    blank_mask,
    norm_gain,
    norm_bias,
    w_qkv,
    qv_bias,
    rel_bias,
    w_out,
    out_bias,
    w_up,
    up_bias,
    w_down,
    grad_out,
):
    tensor_count = lax.axis_size("tensor")
    rows_all = tokens.shape[0]
    rows_own = rows_all // tensor_count
    row_start = lax.axis_index("tensor") * rows_own
    window_area = WS * WS
    windows = rows_all // window_area
    heads_here = rel_bias.shape[0]
    width_here = w_out.shape[0]
    head_dim = width_here // heads_here
    score_scale = head_dim ** (-0.5)

    def own_rows(values):
        return lax.dynamic_slice_in_dim(values, row_start, rows_own, 0)

    source = tokens.astype(jnp.float32)
    hat_one, inv_one = normalize(source)
    normed_one = (hat_one * norm_gain[0] + norm_bias[0]).astype(jnp.bfloat16)
    projected = jnp.einsum("rd,tde->tre", normed_one, w_qkv, preferred_element_type=jnp.float32)
    shifts = jnp.stack([qv_bias[0], jnp.zeros_like(qv_bias[0]), qv_bias[1]])
    projected = (projected + shifts[:, None, :]).astype(jnp.bfloat16)
    projected = projected.reshape(3, windows, window_area, heads_here, head_dim)
    query_part, key_part, value_part = (projected[0], projected[1], projected[2])
    bias_block = relative(rel_bias, WS)

    def scores_of():
        raw_scores = jnp.einsum(
            "wihc,wjhc->whij", query_part, key_part, preferred_element_type=jnp.float32
        )
        return raw_scores * score_scale + bias_block[None]

    scores = scores_of()
    row_top = jnp.max(scores, axis=-1, keepdims=True)
    exponent = jnp.exp(scores - row_top)
    row_total = jnp.sum(exponent, axis=-1, keepdims=True)
    log_total = row_top + jnp.log(row_total)
    weights = (exponent / row_total).astype(jnp.bfloat16)
    mixed_heads = jnp.einsum(
        "whij,wjhc->wihc", weights, value_part, preferred_element_type=jnp.float32
    )
    mixed_heads = mixed_heads.astype(jnp.bfloat16).reshape(rows_all, width_here)
    attn_part = jnp.dot(mixed_heads, w_out, preferred_element_type=jnp.float32)
    alive_rows = jnp.repeat(1.0 - blank_mask.astype(jnp.float32), window_area)
    alive_own = own_rows(alive_rows)[:, None]
    source_own = own_rows(source)
    attn_own = scatter_rows(attn_part) + out_bias[0]
    resid_own = source_own + attn_own
    hat_two, inv_two = normalize(resid_own)
    normed_rows = (hat_two * norm_gain[1] + norm_bias[1]).astype(jnp.bfloat16)
    normed_two = lax.all_gather(normed_rows, "tensor", axis=0, tiled=True)
    hidden = jnp.dot(normed_two, w_up, preferred_element_type=jnp.float32) + up_bias
    active = jax.nn.gelu(hidden, approximate=False).astype(jnp.bfloat16)
    mlp_part = jnp.dot(active, w_down, preferred_element_type=jnp.float32)
    branch_own = scatter_rows(mlp_part) + out_bias[1]
    output = (resid_own + branch_own).astype(jnp.bfloat16)
    stat_terms = jnp.stack(
        [
            jnp.sum(alive_own * source_own * source_own),
            jnp.sum(alive_own * attn_own * attn_own),
            jnp.sum(alive_own * branch_own * branch_own),
            jnp.sum(alive_own),
        ]
    )
    stat_total = lax.psum(stat_terms, ("dp", "tensor"))
    grad_full = grad_out.astype(jnp.float32)
    grad_down = jnp.einsum("rf,rd->fd", active, grad_out, preferred_element_type=jnp.float32)
    grad_active = jnp.einsum("rd,fd->rf", grad_out, w_down, preferred_element_type=jnp.float32)
    gelu_slope = (
        0.5 * (1.0 + lax.erf(hidden * half_root))
        + hidden * jnp.exp(-0.5 * hidden * hidden) * gauss_norm
    )
    grad_hidden = (grad_active * gelu_slope).astype(jnp.bfloat16)
    grad_up_bias = jnp.sum(grad_hidden.astype(jnp.float32), axis=0)
    grad_up = jnp.einsum("rd,rf->df", normed_two, grad_hidden, preferred_element_type=jnp.float32)
    norm_part = jnp.einsum("rf,df->rd", grad_hidden, w_up, preferred_element_type=jnp.float32)
    grad_norm_own = scatter_rows(norm_part)
    grad_resid_own = own_rows(grad_full) + norm_back(grad_norm_own, hat_two, inv_two, norm_gain[1])
    grad_attn = lax.all_gather(grad_resid_own.astype(jnp.bfloat16), "tensor", axis=0, tiled=True)
    gain_two = jnp.sum(grad_norm_own * hat_two, axis=0)
    shift_two = jnp.sum(grad_norm_own, axis=0)
    attn_bias_term = jnp.sum(own_rows(grad_attn).astype(jnp.float32), axis=0)
    mlp_bias_term = jnp.sum(own_rows(grad_full), axis=0)
    grad_wout = jnp.einsum("re,rd->ed", mixed_heads, grad_attn, preferred_element_type=jnp.float32)
    grad_mixed = jnp.einsum("rd,ed->re", grad_attn, w_out, preferred_element_type=jnp.float32)
    grad_mixed = grad_mixed.astype(jnp.bfloat16).reshape(windows, window_area, heads_here, head_dim)
    probs_full = jnp.exp(scores_of() - log_total)
    probs_low = probs_full.astype(jnp.bfloat16)
    grad_values = jnp.einsum(
        "whij,wihc->wjhc", probs_low, grad_mixed, preferred_element_type=jnp.float32
    )
    grad_probs = jnp.einsum(
        "wihc,wjhc->whij", grad_mixed, value_part, preferred_element_type=jnp.float32
    )
    inner_sum = jnp.sum(grad_probs * probs_full, axis=-1, keepdims=True)
    grad_scores = (probs_full * (grad_probs - inner_sum)).astype(jnp.bfloat16)
    grad_table = relative_back(jnp.sum(grad_scores.astype(jnp.float32), axis=0), WS)
    grad_query = (
        jnp.einsum("whij,wjhc->wihc", grad_scores, key_part, preferred_element_type=jnp.float32)
        * score_scale
    )
    grad_keys = (
        jnp.einsum("whij,wihc->wjhc", grad_scores, query_part, preferred_element_type=jnp.float32)
        * score_scale
    )
    grad_proj = (
        jnp.stack([grad_query, grad_keys, grad_values])
        .astype(jnp.bfloat16)
        .reshape(3, rows_all, width_here)
    )
    grad_qv = jnp.stack(
        [
            jnp.sum(grad_proj[0].astype(jnp.float32), axis=0),
            jnp.sum(grad_proj[2].astype(jnp.float32), axis=0),
        ]
    )
    grad_qkv = jnp.einsum("rd,tre->tde", normed_one, grad_proj, preferred_element_type=jnp.float32)
    input_part = jnp.einsum("tre,tde->rd", grad_proj, w_qkv, preferred_element_type=jnp.float32)
    grad_in_own = scatter_rows(input_part)
    hat_one_own = own_rows(hat_one)
    grad_tokens = grad_resid_own + norm_back(
        grad_in_own, hat_one_own, own_rows(inv_one), norm_gain[0]
    )
    gain_one = jnp.sum(grad_in_own * hat_one_own, axis=0)
    shift_one = jnp.sum(grad_in_own, axis=0)
    gain_terms = jnp.stack([gain_one, gain_two])
    shift_terms = jnp.stack([shift_one, shift_two])
    bias_terms = jnp.stack([attn_bias_term, mlp_bias_term])
    gain_sums, shift_sums, bias_sums = lax.psum(
        (gain_terms, shift_terms, bias_terms), ("dp", "tensor")
    )
    grad_qv, grad_table, grad_up_bias = lax.psum((grad_qv, grad_table, grad_up_bias), "dp")
    grad_qkv, grad_wout, grad_up, grad_down = [
        total.astype(jnp.float32)
        for total in lax.psum(
            [part.astype(jnp.bfloat16) for part in (grad_qkv, grad_wout, grad_up, grad_down)], "dp"
        )
    ]
    live_count = jnp.maximum(stat_total[3], 1.0) * tokens.shape[1]
    root_means = jnp.sqrt(stat_total[0:3] / live_count)
    return (
        output,
        grad_tokens,
        gain_sums,
        shift_sums,
        grad_qkv,
        grad_qv,
        grad_table,
        grad_wout,
        bias_sums,
        grad_up,
        grad_up_bias,
        grad_down,
        root_means,
    )


def solution(mesh):
    in_specs = (
        P("dp", None),
        P("dp"),
        P(),
        P(),
        P(None, None, "tensor"),
        P(None, "tensor"),
        P("tensor", None),
        P("tensor", None),
        P(),
        P(None, "tensor"),
        P("tensor"),
        P("tensor", None),
        P("dp", None),
    )
    out_specs = (
        P(("dp", "tensor"), None),
        P(("dp", "tensor"), None),
        P(),
        P(),
        P(None, None, "tensor"),
        P(None, "tensor"),
        P("tensor", None),
        P("tensor", None),
        P(),
        P(None, "tensor"),
        P("tensor"),
        P("tensor", None),
        P(),
    )
    return jax.shard_map(
        on_device, mesh=mesh, in_specs=in_specs, out_specs=out_specs, check_vma=False
    )
```

profile of v0, /device:TPU:0, one launch (start us, length us, event | category | flops | bytes accessed | tf_op | source)
XLA Modules:
  0.0 476.1 jit_solution(3866228508899291969)
XLA Ops:
  8.7 4.8 %convolution_bitcast_fusion = f32[8,10,10,10,10]{4,3,2,1,0:T(8,128)} fusion(f32[8,19,10,10,1]{1,3,4,2,0:T(8,128)S(1)} %convolution_bitcast_fusion.2, s32[10,10]{1,0:T(8,128)S(1)} %subtract_add_fusion), kind=kOutput, calls=%fused_computation.39 | convolution fusion | flops 18241900 | bytes 381200 | tf_op jit(solution)/shard_map/ija,klb,hab->hikjl/dot_general | solution.py:40
  13.5 4.4 reshape.173
  42.8 3.5 convert_element_type.123
  46.4 35.6 %reduce-scatter.5.cloned.1.call-done = bf16[200,1024]{1,0:T(8,128)(2,1)} async-done(((bf16[800,1024]{1,0:T(8,128)(2,1)}), bf16[200,1024]{1,0:T(8,128)(2,1)}) %reduce-scatter.5.cloned.1.call-update) | async-done | bytes 409616 | tf_op jit(solution)/shard_map/reduce_scatter | solution.py:53
  84.7 37.1 %all-gather.3.cloned.1.call-done = bf16[800,1024]{1,0:T(8,128)(2,1)} async-done(((bf16[200,1024]{1,0:T(8,128)(2,1)}), bf16[800,1024]{1,0:T(8,128)(2,1)}) %all-gather.3.cloned.1.call-update) | async-done | bytes 1638416 | tf_op jit(solution)/shard_map/all_gather | solution.py:120
  121.8 10.8 %fusion.2 = (bf16[800,1024]{1,0:T(8,128)(2,1)}, f32[800,1024]{1,0:T(8,128)S(1)}) fusion(f32[1024]{0:T(1024)S(1)} %copy-done.50, bf16[800,1024]{1,0:T(8,128)(2,1)} %all-gather.3.cloned.1.call-done, bf16[1024,1024]{1,0:T(8,128)(2,1)S(1)} %copy-done), kind=kOutput, calls=%fused_computation.11 | convolution fusion | flops 1731788800 | bytes 8654848 | tf_op jit(solution)/shard_map/dot_general | solution.py:121
  132.7 3.7 convert_reduce_fusion.1
  140.7 5.3 %convolution_convert_fusion.4 = bf16[800,1024]{1,0:T(8,128)(2,1)} fusion(bf16[800,1024]{1,0:T(8,128)(2,1)} %get-tuple-element.100, bf16[1024,1024]{1,0:T(8,128)(2,1)} %param.24), kind=kOutput, calls=%fused_computation.47 | convolution fusion | flops 1678540800 | bytes 5373952 | tf_op jit(solution)/shard_map/dot_general | solution.py:123
  146.9 29.1 %reduce-scatter.9.cloned.1.call-done = bf16[200,1024]{1,0:T(8,128)(2,1)} async-done(((bf16[800,1024]{1,0:T(8,128)(2,1)}), bf16[200,1024]{1,0:T(8,128)(2,1)}) %reduce-scatter.9.cloned.1.call-update) | async-done | bytes 409616 | tf_op jit(solution)/shard_map/reduce_scatter | solution.py:53
  178.1 35.5 %reduce-scatter.7.cloned.1.call-done = bf16[200,1024]{1,0:T(8,128)(2,1)} async-done(((bf16[800,1024]{1,0:T(8,128)(2,1)}), bf16[200,1024]{1,0:T(8,128)(2,1)}) %reduce-scatter.7.cloned.1.call-update) | async-done | bytes 409616 | tf_op jit(solution)/shard_map/reduce_scatter | solution.py:53
  213.6 3.8 fusion.81
  217.8 5.3 %convolution_convert_fusion = bf16[1024,1024]{1,0:T(8,128)(2,1)} fusion(bf16[800,1024]{1,0:T(8,128)(2,1)} %get-tuple-element.100, bf16[800,1024]{1,0:T(8,128)(2,1)S(1)} %copy-done.26), kind=kOutput, calls=%fused_computation.43 | convolution fusion | flops 1678770176 | bytes 5373952 | tf_op jit(solution)/shard_map/rf,rd->fd/dot_general | solution.py:136
  223.1 3.7 convolution_convert_fusion.1
  226.8 27.8 %all-gather.5.cloned.1.call-done = bf16[800,1024]{1,0:T(8,128)(2,1)} async-done(((bf16[200,1024]{1,0:T(8,128)(2,1)}), bf16[800,1024]{1,0:T(8,128)(2,1)}) %all-gather.5.cloned.1.call-update) | async-done | bytes 1638416 | tf_op jit(solution)/shard_map/all_gather | solution.py:148
  275.1 4.4 fusion.23
  282.0 4.1 bitcast_convert_fusion
  291.1 4.0 reshape.174
  295.1 12.4 %copy.101 = f32[8,10,10,10,10]{4,3,1,2,0:T(8,128)} copy(f32[8,10,10,10,10]{2,1,4,3,0:T(8,128)} %reshape.174) | data formatting | bytes 640000 | tf_op jit(solution)/shard_map/reshape | solution.py:47
  307.4 8.3 %convolution_bitcast_fusion.1 = f32[19,8,10,10]{0,3,2,1:T(8,128)S(1)} fusion(f32[8,10,10,10,10]{4,3,1,2,0:T(8,128)} %copy.101, s32[10,10]{1,0:T(8,128)S(1)} %copy-done.24), kind=kOutput, calls=%fused_computation.62 | convolution fusion | flops 18241900 | bytes 381200 | tf_op jit(solution)/shard_map/hikjl,ija,klb->hab/dot_general | solution.py:48
  316.5 25.3 %all-reduce.1 = (f32[2,256]{1,0:T(2,128)}, f32[8,361]{1,0:T(8,128)}, f32[1024]{0:T(1024)}) all-reduce(f32[2,256]{1,0:T(2,128)S(1)} %pad_maximum_fusion.7, f32[8,361]{1,0:T(8,128)S(1)} %reshape.160, f32[1024]{0:T(1024)S(1)} %copy-done.45), channel_id=1, replica_groups=mesh['dp'=8,'tensor'=4] {'dp'}, use_global_device_ids=true, to_apply=%region_24.0 | all-reduce | flops 4424 | bytes 35392 | tf_op jit(solution)/shard_map/psum | solution.py:201
  341.8 42.5 %all-reduce.5.cloned.1.call-done = (bf16[3,1024,256]{1,2,0:T(8,128)(2,1)}, bf16[256,1024]{1,0:T(8,128)(2,1)}, bf16[1024,1024]{1,0:T(8,128)(2,1)}, bf16[1024,1024]{1,0:T(8,128)(2,1)}) async-done(((bf16[3,1024,256]{1,2,0:T(8,128)(2,1)}, bf16[256,1024]{1,0:T(8,128)(2,1)}, bf16[1024,1024]{1,0:T(8,128)(2,1)}, bf16[1024,1024]{1,0:T(8,128)(2,1)}), (bf16[3,1024,256]{1,2,0:T(8,128)(2,1)}, ...) | async-done | bytes 6291472 | tf_op jit(solution)/shard_map/psum | solution.py:204
  384.4 3.2 copy.93
  393.7 29.6 %reduce-scatter.11.cloned.1.call-done = bf16[200,1024]{1,0:T(8,128)(2,1)} async-done(((bf16[800,1024]{1,0:T(8,128)(2,1)}), bf16[200,1024]{1,0:T(8,128)(2,1)}) %reduce-scatter.11.cloned.1.call-update) | async-done | bytes 409616 | tf_op jit(solution)/shard_map/reduce_scatter | solution.py:53
  425.1 39.7 %all-reduce = (f32[2,1024]{1,0:T(2,128)}, f32[2,1024]{1,0:T(2,128)}, f32[2,1024]{1,0:T(2,128)}, f32[4]{0:T(128)S(1)}) all-reduce(f32[2,1024]{1,0:T(2,128)S(1)} %pad_maximum_fusion.3, f32[2,1024]{1,0:T(2,128)S(1)} %pad_maximum_fusion.4, f32[2,1024]{1,0:T(2,128)S(1)} %pad_maximum_fusion.5, ...), channel_id=1, replica_groups=mesh['dp'=8,'tensor'=4] {'dp','tensor'}, use_global_device_ids=true, to_apply=%region_17.0 | all-reduce | flops 6148 | bytes 49184 | tf_op jit(solution)/shard_map/psum | solution.py:198
  (202 shorter events, 76.4 us)
Async XLA Ops:
  7.2 114.6 %copy-start = (bf16[1024,1024]{1,0:T(8,128)(2,1)S(1)}, bf16[1024,1024]{1,0:T(8,128)(2,1)}, u32[]{:S(2)}) copy-start(bf16[1024,1024]{1,0:T(8,128)(2,1)} %param.22) | copy-start | bytes 6291460
  7.2 74.7 %reduce-scatter.5.cloned.1.call-start = ((), (), s32[]{:S(2)}) async-start(), calls=%async_computation.4 | async-start | bytes 2048000 | tf_op jit(solution)/shard_map/reduce_scatter | solution.py:53
  27.6 9.5 %copy-start.6 = (bf16[8,100,8,32]{1,0,3,2:T(8,128)(2,1)}, bf16[8,100,8,32]{1,0,3,2:T(8,128)(2,1)S(1)}, u32[]{:S(2)}) copy-start(bf16[8,100,8,32]{1,0,3,2:T(8,128)(2,1)S(1)} %squeeze.14) | copy-start | bytes 1228804
  42.6 41.1 %copy-start.28 = (f32[1,1024]{1,0:T(1,128)S(1)}, f32[1,1024]{1,0:T(1,128)}, u32[]{:S(2)}) copy-start(f32[1,1024]{1,0:T(1,128)} %get-tuple-element.92) | copy-start | bytes 12292
  42.6 41.1 %copy-start.39 = (f32[1,1024]{1,0:T(1,128)S(1)}, f32[1,1024]{1,0:T(1,128)}, u32[]{:S(2)}) copy-start(f32[1,1024]{1,0:T(1,128)} %get-tuple-element.94) | copy-start | bytes 12292
  42.6 79.2 %all-gather.3.cloned.1.call-start = ((), (), s32[]{:S(2)}) async-start(), calls=%async_computation.5 | async-start | bytes 2048000 | tf_op jit(solution)/shard_map/all_gather | solution.py:120
  46.4 75.5 %copy-start.50 = (f32[1024]{0:T(1024)S(1)}, f32[1024]{0:T(1024)}, u32[]{:S(2)}) copy-start(f32[1024]{0:T(1024)} %param.23) | copy-start | bytes 12292
  84.7 91.4 %reduce-scatter.9.cloned.1.call-start = ((), (), s32[]{:S(2)}) async-start(), calls=%async_computation.7 | async-start | bytes 2048000 | tf_op jit(solution)/shard_map/reduce_scatter | solution.py:53
  121.8 10.8 %copy-start.25 = (bf16[800,1024]{1,0:T(8,128)(2,1)S(1)}, bf16[800,1024]{1,0:T(8,128)(2,1)}, u32[]{:S(2)}) copy-start(bf16[800,1024]{1,0:T(8,128)(2,1)} %param.25) | copy-start | bytes 4915204
  121.8 10.8 %copy-start.47 = (bf16[1024,1024]{1,0:T(8,128)(2,1)S(1)}, bf16[1024,1024]{1,0:T(8,128)(2,1)}, u32[]{:S(2)}) copy-start(bf16[1024,1024]{1,0:T(8,128)(2,1)} %param.24) | copy-start | bytes 6291460
  140.6 73.0 %reduce-scatter.7.cloned.1.call-start = ((), (), s32[]{:S(2)}) async-start(), calls=%async_computation.6 | async-start | bytes 2048000 | tf_op jit(solution)/shard_map/reduce_scatter | solution.py:53
  140.7 72.9 %copy-start.19 = (bf16[200,1024]{1,0:T(8,128)(2,1)S(1)}, bf16[200,1024]{1,0:T(8,128)(2,1)}, u32[]{:S(2)}) copy-start(bf16[200,1024]{1,0:T(8,128)(2,1)} %reduce-scatter.5.cloned.1.call-done) | copy-start | bytes 1228804
  140.7 72.9 %copy-start.26 = (bf16[800,1024]{1,0:T(8,128)(2,1)S(1)}, bf16[800,1024]{1,0:T(8,128)(2,1)}, u32[]{:S(2)}) copy-start(bf16[800,1024]{1,0:T(8,128)(2,1)} %param.25) | copy-start | bytes 4915204
  146.0 108.6 %all-gather.5.cloned.1.call-start = ((), (), s32[]{:S(2)}) async-start(), calls=%async_computation.8 | async-start | bytes 2048000 | tf_op jit(solution)/shard_map/all_gather | solution.py:148
  217.5 166.9 %all-reduce.5.cloned.1.call-start = ((), (), s32[]{:S(2)}) async-start(), calls=%async_computation.10 | async-start | bytes 12582912 | tf_op jit(solution)/shard_map/psum | solution.py:204
  226.8 35.2 %copy-start.3 = (f32[8,8,100,100]{2,3,1,0:T(8,128)S(1)}, f32[8,8,100,100]{2,3,1,0:T(8,128)}, u32[]{:S(2)}) copy-start(f32[8,8,100,100]{2,3,1,0:T(8,128)} %copy-done.2) | copy-start | bytes 7680004
  281.1 142.2 %reduce-scatter.11.cloned.1.call-start = ((), (), s32[]{:S(2)}) async-start(), calls=%async_computation.9 | async-start | bytes 2048000 | tf_op jit(solution)/shard_map/reduce_scatter | solution.py:53
  295.1 12.4 %copy-start.24 = (s32[10,10]{1,0:T(8,128)S(1)}, s32[10,10]{1,0:T(8,128)}, u32[]{:S(2)}) copy-start(s32[10,10]{1,0:T(8,128)} %copy-done.23) | copy-start | bytes 1204
  391.2 32.1 %copy-start.32 = (f32[1,1024]{1,0:T(1,128)S(1)}, f32[1,1024]{1,0:T(1,128)}, u32[]{:S(2)}) copy-start(f32[1,1024]{1,0:T(1,128)} %copy-done.31) | copy-start | bytes 12292
  391.2 33.9 %copy-start.38 = (f32[1024]{0:T(1024)S(1)}, f32[1024]{0:T(1024)}, u32[]{:S(2)}) copy-start(f32[1024]{0:T(1024)} %get-tuple-element.54) | copy-start | bytes 12292
  391.2 33.9 %copy-start.37 = (f32[1024]{0:T(1024)S(1)}, f32[1024]{0:T(1024)}, u32[]{:S(2)}) copy-start(f32[1024]{0:T(1024)} %get-tuple-element.59) | copy-start | bytes 12292
  391.2 33.9 %copy-start.40 = (f32[1024]{0:T(1024)S(1)}, f32[1024]{0:T(1024)}, u32[]{:S(2)}) copy-start(f32[1024]{0:T(1024)} %get-tuple-element.82) | copy-start | bytes 12292
  391.2 75.4 %copy-start.11 = (f32[200,1024]{1,0:T(8,128)S(1)}, f32[200,1024]{1,0:T(8,128)}, u32[]{:S(2)}) copy-start(f32[200,1024]{1,0:T(8,128)} %get-tuple-element.79) | copy-start | bytes 2457604
  391.2 77.8 %copy-start.1 = (bf16[1024,1024]{1,0:T(8,128)(2,1)S(1)}, bf16[1024,1024]{1,0:T(8,128)(2,1)}, u32[]{:S(2)}) copy-start(bf16[1024,1024]{1,0:T(8,128)(2,1)} %param.22) | copy-start | bytes 6291460
  (37 other events, 154.3 us)
Sparse Core Ops, SparseCore 0:
  42.7 39.1 reduce-scatter.4
  84.8 36.9 all-gather.2
  140.7 35.2 reduce-scatter.8
  178.2 35.3 reduce-scatter.6
  217.6 36.9 all-gather.4
  281.2 103.1 all-reduce.4
  386.7 36.5 reduce-scatter.10
where the time goes:
time: 485 us; the launch traced here: 476 us
  waiting for transfers between devices  237 us (49%)
  matrix products  73 us (15%)
  blocking collectives  65 us (13%)
  local copies, waits for them, and re-layouts  49.5 us (10%)
  other arithmetic  34.9 us (7%)
  between operations  15.6 us (3%)
    reduce_scatter x4, waiting for transfers between devices, scatter_rows(): lax.psum_scatter(part.astype(jnp.bfloat16), 'tensor', scatter_dimension=0...  130 us
    psum x1, waiting for transfers between devices, on_device(): lax.psum([part.astype(jnp.bfloat16) for part in (grad_qkv, grad_wout, gra...  42.5 us
    psum x1, blocking collectives, on_device(): lax.psum((gain_terms, shift_terms, bias_terms), ('dp', 'tensor'))  39.7 us
    all_gather x1, waiting for transfers between devices, on_device(): normed_two = lax.all_gather(normed_rows, 'tensor', axis=0, tiled=True)  37.1 us
    all_gather x1, waiting for transfers between devices, on_device(): lax.all_gather(grad_resid_own.astype(jnp.bfloat16), 'tensor', axis=0, til...  27.8 us
    psum x1, blocking collectives, on_device(): lax.psum((grad_qv, grad_table, grad_up_bias), 'dp')  25.3 us
    reshape x2, local copies, waits for them, and re-layouts, relative_back(): gradient.reshape(heads_count, window_side, window_side, window_side, wind...  16.3 us
    dot_general x1, matrix products, on_device(): jnp.dot(normed_two, w_up, preferred_element_type=jnp.float32) + up_bias  10.8 us
  transfers between devices with their start and end apart: 7, of which 7 were waited for; matrix products, arithmetic and copies ran while one was open for 14% of the time, Pallas kernels for 0%

commit v1 on v0

--- a/solution.py
+++ b/solution.py
@@ -8,6 +8,21 @@
 norm_eps = 1e-05
 half_root = 0.7071067811865476
 gauss_norm = 0.3989422804014327
+
+
+def press_vectors(shard_in, lane_axis):
+    low = jax.lax.psum(1, axis_name=lane_axis)
+    val2 = jax.lax.axis_index(lane_axis)
+    finding, fresh, t_next = (low, val2, shard_in.shape[0])
+    y2 = jnp.zeros((*shard_in.shape[:0], finding * t_next, *shard_in.shape[1:]), shard_in.dtype)
+    blocks_here = tuple(((it, (it + 1) % finding) for it in range(finding)))
+    view_out = shard_in
+    for c in range(finding):
+        last = (fresh - c) % finding
+        y2 = lax.dynamic_update_slice_in_dim(y2, view_out, last * t_next, axis=0)
+        if c < finding - 1:
+            view_out = jax.lax.ppermute(view_out, axis_name=lane_axis, perm=blocks_here)
+    return y2
 
 
 def normalize(values):
@@ -145,7 +160,7 @@
     norm_part = jnp.einsum("rf,df->rd", grad_hidden, w_up, preferred_element_type=jnp.float32)
     grad_norm_own = scatter_rows(norm_part)
     grad_resid_own = own_rows(grad_full) + norm_back(grad_norm_own, hat_two, inv_two, norm_gain[1])
-    grad_attn = lax.all_gather(grad_resid_own.astype(jnp.bfloat16), "tensor", axis=0, tiled=True)
+    grad_attn = press_vectors(grad_resid_own.astype(jnp.bfloat16), lane_axis="tensor")
     gain_two = jnp.sum(grad_norm_own * hat_two, axis=0)
     shift_two = jnp.sum(grad_norm_own, axis=0)
     attn_bias_term = jnp.sum(own_rows(grad_attn).astype(jnp.float32), axis=0)

time: 485 us -> 488 us (level)
    all_gather x1 -> x0, waiting for transfers between devices: 27.8 us -> none  [on_device(): lax.all_gather(grad_resid_own.astype(jnp.bfloat16), 'tensor', axis=0, til...]
    ppermute x0 -> x3, waiting for transfers between devices: none -> 24.5 us  [press_vectors(): view_out = jax.lax.ppermute(view_out, axis_name=lane_axis, perm=blocks_here)]
  transfers between devices with their start and end apart: 7 -> 9, of which waited for: 7 -> 9; matrix products, arithmetic and copies ran while one was open for 14% -> 14% of each run, Pallas kernels for 0% -> 0%
where the time goes in v1:
time: 488 us; the launch traced here: 479 us
  waiting for transfers between devices  236 us (48%)
  matrix products  74.1 us (15%)
  blocking collectives  63.6 us (13%)
  local copies, waits for them, and re-layouts  52.8 us (11%)
  other arithmetic  35.9 us (7%)
  between operations  15.6 us (3%)
    reduce_scatter x4, waiting for transfers between devices, scatter_rows(): lax.psum_scatter(part.astype(jnp.bfloat16), 'tensor', scatter_dimension=0...  132 us
    psum x1, waiting for transfers between devices, on_device(): lax.psum([part.astype(jnp.bfloat16) for part in (grad_qkv, grad_wout, gra...  42.1 us
    psum x1, blocking collectives, on_device(): lax.psum((gain_terms, shift_terms, bias_terms), ('dp', 'tensor'))  39.8 us
    all_gather x1, waiting for transfers between devices, on_device(): normed_two = lax.all_gather(normed_rows, 'tensor', axis=0, tiled=True)  37.1 us
    ppermute x3, waiting for transfers between devices, press_vectors(): view_out = jax.lax.ppermute(view_out, axis_name=lane_axis, perm=blocks_here)  24.5 us
    psum x1, blocking collectives, on_device(): lax.psum((grad_qv, grad_table, grad_up_bias), 'dp')  23.9 us
    reshape x2, local copies, waits for them, and re-layouts, relative_back(): gradient.reshape(heads_count, window_side, window_side, window_side, wind...  16.3 us
    dot_general x1, matrix products, on_device(): jnp.dot(normed_two, w_up, preferred_element_type=jnp.float32) + up_bias  10.8 us
  transfers between devices with their start and end apart: 9, of which 9 were waited for; matrix products, arithmetic and copies ran while one was open for 14% of the time, Pallas kernels for 0%

profile of v1, /device:TPU:0, one launch (start us, length us, event | category | flops | bytes accessed | tf_op | source)
XLA Modules:
  0.0 478.7 jit_solution(6745564054370685773)
XLA Ops:
  8.7 4.8 %convolution_bitcast_fusion = f32[8,10,10,10,10]{4,3,2,1,0:T(8,128)} fusion(f32[8,19,10,10,1]{1,3,4,2,0:T(8,128)S(1)} %convolution_bitcast_fusion.2, s32[10,10]{1,0:T(8,128)S(1)} %subtract_add_fusion), kind=kOutput, calls=%fused_computation.39 | convolution fusion | flops 18241900 | bytes 381200 | tf_op jit(solution)/shard_map/ija,klb,hab->hikjl/dot_general | solution.py:55
  13.5 4.4 reshape.173
  42.8 3.5 convert_element_type.123
  46.4 35.5 %reduce-scatter.5.cloned.1.call-done = bf16[200,1024]{1,0:T(8,128)(2,1)} async-done(((bf16[800,1024]{1,0:T(8,128)(2,1)}), bf16[200,1024]{1,0:T(8,128)(2,1)}) %reduce-scatter.5.cloned.1.call-update) | async-done | bytes 409616 | tf_op jit(solution)/shard_map/reduce_scatter | solution.py:68
  84.7 37.1 %all-gather.2.cloned.1.call-done = bf16[800,1024]{1,0:T(8,128)(2,1)} async-done(((bf16[200,1024]{1,0:T(8,128)(2,1)}), bf16[800,1024]{1,0:T(8,128)(2,1)}) %all-gather.2.cloned.1.call-update) | async-done | bytes 1638416 | tf_op jit(solution)/shard_map/all_gather | solution.py:135
  121.8 10.8 %fusion.2 = (bf16[800,1024]{1,0:T(8,128)(2,1)}, f32[800,1024]{1,0:T(8,128)S(1)}) fusion(f32[1024]{0:T(1024)S(1)} %copy-done.50, bf16[800,1024]{1,0:T(8,128)(2,1)} %all-gather.2.cloned.1.call-done, bf16[1024,1024]{1,0:T(8,128)(2,1)S(1)} %copy-done), kind=kOutput, calls=%fused_computation.11 | convolution fusion | flops 1731788800 | bytes 8654848 | tf_op jit(solution)/shard_map/dot_general | solution.py:136
  132.6 3.7 convert_reduce_fusion.1
  140.7 5.2 %convolution_convert_fusion.4 = bf16[800,1024]{1,0:T(8,128)(2,1)} fusion(bf16[800,1024]{1,0:T(8,128)(2,1)} %get-tuple-element.100, bf16[1024,1024]{1,0:T(8,128)(2,1)} %param.24), kind=kOutput, calls=%fused_computation.47 | convolution fusion | flops 1678540800 | bytes 5373952 | tf_op jit(solution)/shard_map/dot_general | solution.py:138
  146.8 29.2 %reduce-scatter.9.cloned.1.call-done = bf16[200,1024]{1,0:T(8,128)(2,1)} async-done(((bf16[800,1024]{1,0:T(8,128)(2,1)}), bf16[200,1024]{1,0:T(8,128)(2,1)}) %reduce-scatter.9.cloned.1.call-update) | async-done | bytes 409616 | tf_op jit(solution)/shard_map/reduce_scatter | solution.py:68
  176.1 37.5 %reduce-scatter.7.cloned.1.call-done = bf16[200,1024]{1,0:T(8,128)(2,1)} async-done(((bf16[800,1024]{1,0:T(8,128)(2,1)}), bf16[200,1024]{1,0:T(8,128)(2,1)}) %reduce-scatter.7.cloned.1.call-update) | async-done | bytes 409616 | tf_op jit(solution)/shard_map/reduce_scatter | solution.py:68
  221.0 12.3 %collective-permute-done = bf16[200,1024]{1,0:T(8,128)(2,1)S(1)} collective-permute-done((bf16[200,1024]{1,0:T(8,128)(2,1)S(1)}, bf16[200,1024]{1,0:T(8,128)(2,1)S(1)}, u32[]{:S(2)}, u32[]{:S(2)}) %collective-permute-start) | collective-permute-done | bytes 409632 | tf_op jit(solution)/shard_map/ppermute | solution.py:24
  233.4 5.1 %convolution_convert_fusion = bf16[1024,1024]{1,0:T(8,128)(2,1)} fusion(bf16[800,1024]{1,0:T(8,128)(2,1)} %get-tuple-element.100, bf16[800,1024]{1,0:T(8,128)(2,1)S(1)} %copy-done.24), kind=kOutput, calls=%fused_computation.43 | convolution fusion | flops 1678770176 | bytes 5373952 | tf_op jit(solution)/shard_map/rf,rd->fd/dot_general | solution.py:151
  238.5 6.6 %collective-permute-done.1 = bf16[200,1024]{1,0:T(8,128)(2,1)S(1)} collective-permute-done((bf16[200,1024]{1,0:T(8,128)(2,1)S(1)}, bf16[200,1024]{1,0:T(8,128)(2,1)S(1)}, u32[]{:S(2)}, u32[]{:S(2)}) %collective-permute-start.1) | collective-permute-done | bytes 409632 | tf_op jit(solution)/shard_map/ppermute | solution.py:24
  245.5 3.7 convolution_convert_fusion.1
  250.9 5.5 %collective-permute-done.2 = bf16[200,1024]{1,0:T(8,128)(2,1)S(1)} collective-permute-done((bf16[200,1024]{1,0:T(8,128)(2,1)S(1)}, bf16[200,1024]{1,0:T(8,128)(2,1)S(1)}, u32[]{:S(2)}, u32[]{:S(2)}) %collective-permute-start.2) | collective-permute-done | bytes 409632 | tf_op jit(solution)/shard_map/ppermute | solution.py:24
  280.1 4.4 fusion.23
  285.5 4.1 bitcast_convert_fusion
  295.7 4.0 reshape.174
  299.7 12.3 %copy.101 = f32[8,10,10,10,10]{4,3,1,2,0:T(8,128)} copy(f32[8,10,10,10,10]{2,1,4,3,0:T(8,128)} %reshape.174) | data formatting | bytes 640000 | tf_op jit(solution)/shard_map/reshape | solution.py:62
  312.0 8.3 %convolution_bitcast_fusion.1 = f32[19,8,10,10]{0,3,2,1:T(8,128)S(1)} fusion(f32[8,10,10,10,10]{4,3,1,2,0:T(8,128)} %copy.101, s32[10,10]{1,0:T(8,128)S(1)} %copy-done.28), kind=kOutput, calls=%fused_computation.62 | convolution fusion | flops 18241900 | bytes 381200 | tf_op jit(solution)/shard_map/hikjl,ija,klb->hab/dot_general | solution.py:63
  321.1 23.9 %all-reduce.1 = (f32[2,256]{1,0:T(2,128)}, f32[8,361]{1,0:T(8,128)}, f32[1024]{0:T(1024)}) all-reduce(f32[2,256]{1,0:T(2,128)S(1)} %pad_maximum_fusion.7, f32[8,361]{1,0:T(8,128)S(1)} %reshape.160, f32[1024]{0:T(1024)S(1)} %copy-done.45), channel_id=1, replica_groups=mesh['dp'=8,'tensor'=4] {'dp'}, use_global_device_ids=true, to_apply=%region_24.25 | all-reduce | flops 4424 | bytes 35392 | tf_op jit(solution)/shard_map/psum | solution.py:216
  345.0 42.1 %all-reduce.5.cloned.1.call-done = (bf16[3,1024,256]{1,2,0:T(8,128)(2,1)}, bf16[256,1024]{1,0:T(8,128)(2,1)}, bf16[1024,1024]{1,0:T(8,128)(2,1)}, bf16[1024,1024]{1,0:T(8,128)(2,1)}) async-done(((bf16[3,1024,256]{1,2,0:T(8,128)(2,1)}, bf16[256,1024]{1,0:T(8,128)(2,1)}, bf16[1024,1024]{1,0:T(8,128)(2,1)}, bf16[1024,1024]{1,0:T(8,128)(2,1)}), (bf16[3,1024,256]{1,2,0:T(8,128)(2,1)}, ...) | async-done | bytes 6291472 | tf_op jit(solution)/shard_map/psum | solution.py:219
  396.5 29.4 %reduce-scatter.11.cloned.1.call-done = bf16[200,1024]{1,0:T(8,128)(2,1)} async-done(((bf16[800,1024]{1,0:T(8,128)(2,1)}), bf16[200,1024]{1,0:T(8,128)(2,1)}) %reduce-scatter.11.cloned.1.call-update) | async-done | bytes 409616 | tf_op jit(solution)/shard_map/reduce_scatter | solution.py:68
  427.7 39.8 %all-reduce = (f32[2,1024]{1,0:T(2,128)}, f32[2,1024]{1,0:T(2,128)}, f32[2,1024]{1,0:T(2,128)}, f32[4]{0:T(128)S(1)}) all-reduce(f32[2,1024]{1,0:T(2,128)S(1)} %pad_maximum_fusion.3, f32[2,1024]{1,0:T(2,128)S(1)} %pad_maximum_fusion.4, f32[2,1024]{1,0:T(2,128)S(1)} %pad_maximum_fusion.5, ...), channel_id=1, replica_groups=mesh['dp'=8,'tensor'=4] {'dp','tensor'}, use_global_device_ids=true, to_apply=%region_17.18 | all-reduce | flops 6148 | bytes 49184 | tf_op jit(solution)/shard_map/psum | solution.py:213
  (210 shorter events, 89.6 us)
Async XLA Ops:
  7.2 114.6 %copy-start = (bf16[1024,1024]{1,0:T(8,128)(2,1)S(1)}, bf16[1024,1024]{1,0:T(8,128)(2,1)}, u32[]{:S(2)}) copy-start(bf16[1024,1024]{1,0:T(8,128)(2,1)} %param.22) | copy-start | bytes 6291460
  7.2 74.7 %reduce-scatter.5.cloned.1.call-start = ((), (), s32[]{:S(2)}) async-start(), calls=%async_computation.4 | async-start | bytes 2048000 | tf_op jit(solution)/shard_map/reduce_scatter | solution.py:68
  42.6 41.1 %copy-start.29 = (f32[1,1024]{1,0:T(1,128)S(1)}, f32[1,1024]{1,0:T(1,128)}, u32[]{:S(2)}) copy-start(f32[1,1024]{1,0:T(1,128)} %get-tuple-element.92) | copy-start | bytes 12292
  42.6 41.1 %copy-start.40 = (f32[1,1024]{1,0:T(1,128)S(1)}, f32[1,1024]{1,0:T(1,128)}, u32[]{:S(2)}) copy-start(f32[1,1024]{1,0:T(1,128)} %get-tuple-element.94) | copy-start | bytes 12292
  42.6 79.2 %all-gather.2.cloned.1.call-start = ((), (), s32[]{:S(2)}) async-start(), calls=%async_computation.5 | async-start | bytes 2048000 | tf_op jit(solution)/shard_map/all_gather | solution.py:135
  46.4 75.4 %copy-start.50 = (f32[1024]{0:T(1024)S(1)}, f32[1024]{0:T(1024)}, u32[]{:S(2)}) copy-start(f32[1024]{0:T(1024)} %param.23) | copy-start | bytes 12292
  84.7 91.4 %reduce-scatter.9.cloned.1.call-start = ((), (), s32[]{:S(2)}) async-start(), calls=%async_computation.7 | async-start | bytes 2048000 | tf_op jit(solution)/shard_map/reduce_scatter | solution.py:68
  140.6 73.0 %reduce-scatter.7.cloned.1.call-start = ((), (), s32[]{:S(2)}) async-start(), calls=%async_computation.6 | async-start | bytes 2048000 | tf_op jit(solution)/shard_map/reduce_scatter | solution.py:68
  140.7 72.9 %copy-start.20 = (bf16[200,1024]{1,0:T(8,128)(2,1)S(1)}, bf16[200,1024]{1,0:T(8,128)(2,1)}, u32[]{:S(2)}) copy-start(bf16[200,1024]{1,0:T(8,128)(2,1)} %reduce-scatter.5.cloned.1.call-done) | copy-start | bytes 1228804
  145.9 241.2 %all-reduce.5.cloned.1.call-start = ((), (), s32[]{:S(2)}) async-start(), calls=%async_computation.9 | async-start | bytes 12582912 | tf_op jit(solution)/shard_map/psum | solution.py:219
  176.1 42.3 %copy-start.19 = (bf16[200,1024]{1,0:T(8,128)(2,1)S(1)}, bf16[200,1024]{1,0:T(8,128)(2,1)}, u32[]{:S(2)}) copy-start(bf16[200,1024]{1,0:T(8,128)(2,1)} %reduce-scatter.9.cloned.1.call-done) | copy-start | bytes 1228804
  216.9 16.5 %copy-start.24 = (bf16[800,1024]{1,0:T(8,128)(2,1)S(1)}, bf16[800,1024]{1,0:T(8,128)(2,1)}, u32[]{:S(2)}) copy-start(bf16[800,1024]{1,0:T(8,128)(2,1)} %param.25) | copy-start | bytes 4915204
  220.8 12.6 %collective-permute-start = (bf16[200,1024]{1,0:T(8,128)(2,1)S(1)}, bf16[200,1024]{1,0:T(8,128)(2,1)S(1)}, u32[]{:S(2)}, u32[]{:S(2)}) collective-permute-start(bf16[200,1024]{1,0:T(8,128)(2,1)S(1)} %get-tuple-element.79), channel_id=1, source_target_pairs={{0,1},{1,2},{2,3},{3,0},{4,5},{5,6},{6,7},{7,4},{8,9},{9,10},{10,1... | collective-permute-start | bytes 1228808 | tf_op jit(solution)/shard_map/ppermute | solution.py:24
  221.0 24.5 %copy-start.48 = (bf16[800,1024]{1,0:T(8,128)(2,1)S(1)}, bf16[800,1024]{1,0:T(8,128)(2,1)}, u32[]{:S(2)}) copy-start(bf16[800,1024]{1,0:T(8,128)(2,1)} %all-gather.2.cloned.1.call-done) | copy-start | bytes 4915204
  221.0 24.5 %copy-start.53 = (bf16[800,1024]{1,0:T(8,128)(2,1)S(1)}, bf16[800,1024]{1,0:T(8,128)(2,1)}, u32[]{:S(2)}) copy-start(bf16[800,1024]{1,0:T(8,128)(2,1)} %copy-done.52) | copy-start | bytes 4915204
  233.4 11.7 %collective-permute-start.1 = (bf16[200,1024]{1,0:T(8,128)(2,1)S(1)}, bf16[200,1024]{1,0:T(8,128)(2,1)S(1)}, u32[]{:S(2)}, u32[]{:S(2)}) collective-permute-start(bf16[200,1024]{1,0:T(8,128)(2,1)S(1)} %collective-permute-done), channel_id=1, source_target_pairs={{0,1},{1,2},{2,3},{3,0},{4,5},{5,6},{6,7},{7,4},{8,9},{9,10},{10,1... | collective-permute-start | bytes 1228808 | tf_op jit(solution)/shard_map/ppermute | solution.py:24
  238.5 18.7 %copy-start.21 = (bf16[256,1024]{1,0:T(8,128)(2,1)S(1)}, bf16[256,1024]{1,0:T(8,128)(2,1)}, u32[]{:S(2)}) copy-start(bf16[256,1024]{1,0:T(8,128)(2,1)} %param.20) | copy-start | bytes 1572868
  245.1 11.3 %collective-permute-start.2 = (bf16[200,1024]{1,0:T(8,128)(2,1)S(1)}, bf16[200,1024]{1,0:T(8,128)(2,1)S(1)}, u32[]{:S(2)}, u32[]{:S(2)}) collective-permute-start(bf16[200,1024]{1,0:T(8,128)(2,1)S(1)} %collective-permute-done.1), channel_id=1, source_target_pairs={{0,1},{1,2},{2,3},{3,0},{4,5},{5,6},{6,7},{7,4},{8,9},{9,10},{10,1... | collective-permute-start | bytes 1228808 | tf_op jit(solution)/shard_map/ppermute | solution.py:24
  284.6 141.3 %reduce-scatter.11.cloned.1.call-start = ((), (), s32[]{:S(2)}) async-start(), calls=%async_computation.8 | async-start | bytes 2048000 | tf_op jit(solution)/shard_map/reduce_scatter | solution.py:68
  393.9 31.9 %copy-start.33 = (f32[1,1024]{1,0:T(1,128)S(1)}, f32[1,1024]{1,0:T(1,128)}, u32[]{:S(2)}) copy-start(f32[1,1024]{1,0:T(1,128)} %copy-done.32) | copy-start | bytes 12292
  393.9 33.7 %copy-start.39 = (f32[1024]{0:T(1024)S(1)}, f32[1024]{0:T(1024)}, u32[]{:S(2)}) copy-start(f32[1024]{0:T(1024)} %get-tuple-element.54) | copy-start | bytes 12292
  393.9 33.7 %copy-start.38 = (f32[1024]{0:T(1024)S(1)}, f32[1024]{0:T(1024)}, u32[]{:S(2)}) copy-start(f32[1024]{0:T(1024)} %get-tuple-element.59) | copy-start | bytes 12292
  393.9 75.3 %copy-start.11 = (f32[200,1024]{1,0:T(8,128)S(1)}, f32[200,1024]{1,0:T(8,128)}, u32[]{:S(2)}) copy-start(f32[200,1024]{1,0:T(8,128)} %get-tuple-element.80) | copy-start | bytes 2457604
  394.0 77.7 %copy-start.1 = (bf16[1024,1024]{1,0:T(8,128)(2,1)S(1)}, bf16[1024,1024]{1,0:T(8,128)(2,1)}, u32[]{:S(2)}) copy-start(bf16[1024,1024]{1,0:T(8,128)(2,1)} %param.22) | copy-start | bytes 6291460
  (39 other events, 198.7 us)
Sparse Core Ops, SparseCore 0:
  42.7 39.1 reduce-scatter.4
  84.8 36.9 all-gather.1
  140.7 35.2 reduce-scatter.8
  178.2 35.3 reduce-scatter.6
  284.7 102.4 all-reduce.4
  389.3 36.5 reduce-scatter.10
